TPU v7x, 256 devices: a whole 4x4x8 slice. The times are simulated.
256 devices in a mesh: fac: 32 (over y, z), cust: 8 (over x, core).
Axes of the slice: x: 4, y: 4, z: 8, core: 2. Of those that a mesh axis runs over, the one named last changes fastest.
Arguments:
- fac_coords: bfloat16 [16384, 128], P('fac'), may hold values from -6 to 6
- cust_coords: bfloat16 [131072, 128], P(('cust', 'fac')), may hold values from -6 to 6
- open_flags: int32 [16384], P('fac'), may hold values 0 or 1
- demand: int32 [131072], P('cust'), may hold values from 1 to 4
- fixed_cost: float32 [16384], P('fac'), may hold values from 0 to 64
- capacity: float32 [16384], P('fac'), may hold values from 16 to 64
- cap_mult: float32 [16384], P('fac'), may hold values from 0 to 0.1
- cover_mult: float32 [131072], P('cust'), may hold values from 0 to 2, as said below
Outputs:
- cover_final: float32 [131072], P('cust')
- cap_final: float32 [16384], P('fac')
- bounds: float32 [3], replicated
Inputs may be any that keep to these rules, and one draw needn't show every extreme that they name: `cover_mult`: initial coverage multipliers, all in one band of width 0.4.
All inputs are finite; a program needn't handle non-finite values. No bound on the sum of `open_flags` on one device may be relied on, other than what follows from the above.
Results may differ from a plain program's by a relative error of at most 0.0003.
Values may be sent and summed in bfloat16 or wider, within the bound.
A program may use at most 64 MiB of HBM per device.

v0:
```python
import math

import jax
import jax.numpy as jnp
from jax import lax
from jax.sharding import Mesh
from jax.sharding import PartitionSpec as P

ITERS = 3
FAC = ("fac_0", "fac_1")
CUST_FAC = ("cust", "fac_0", "fac_1")


def laid_out(blocks, dim):
    shape = list(blocks.shape[1:])
    shape[dim] *= blocks.shape[0]
    return jnp.moveaxis(blocks, 0, dim).reshape(shape)


def stacked_from(x, axes, turns):
    blocks = x
    for k in turns:
        blocks = lax.all_gather(blocks, axes[k])
    done = turns[::-1]
    back = [done.index(k) for k in range(len(axes))]
    blocks = blocks.transpose(*back, *range(len(axes), blocks.ndim))
    return blocks.reshape(-1, *x.shape)


def whole_of(x, axes, turns, dim):
    return laid_out(stacked_from(x, axes, turns), dim)


def copy_for_each(x, axis):
    size = lax.axis_size(axis)
    return lax.all_to_all(jnp.broadcast_to(x[None], (size, *x.shape)), axis, 0, 0, tiled=True)


def of_everyone(x, axis):
    everything = copy_for_each(x, axis)
    return jnp.sum(everything, axis=0)


def together(arrays, axis):
    flat, at, done = (jnp.concatenate([a.reshape(-1) for a in arrays]), 0, [])
    total = of_everyone(flat, axis)
    for a in arrays:
        done.append(total[at : at + a.size].reshape(a.shape))
        at += a.size
    return tuple(done)


def grouped_sum(values):
    length = values.shape[-1]
    parts = values.reshape(values.shape[:-1] + (length // 128, 128))
    return jnp.sum(jnp.sum(parts, axis=-1), axis=-1)


def local(fac_coords, cust_coords, open_flags, demand, fixed_cost, capacity, cap_mult, cover_mult):
    tau = 0.1
    coords_all = whole_of(cust_coords, FAC, (0, 1), 0)
    n_cols = coords_all.shape[0]
    width = coords_all.shape[1]
    n_rows = fac_coords.shape[0]
    total_cust = n_cols * lax.axis_size("cust")
    block = math.gcd(n_cols, 2048)
    n_blocks = n_cols // block
    opened = open_flags.astype(jnp.float32)
    weight = demand.astype(jnp.float32)
    pnorm = jnp.sum(fac_coords.astype(jnp.float32) ** 2, axis=1)
    qnorm = jnp.sum(coords_all.astype(jnp.float32) ** 2, axis=1)
    coord_blocks = coords_all.reshape(n_blocks, block, width)
    qnorm_blocks = qnorm.reshape(n_blocks, block)
    weight_blocks = weight.reshape(n_blocks, block)
    lam = cover_mult
    mu = cap_mult
    bound_list = []
    for step in range(ITERS):
        size = 0.1 / (step + 1)
        lam_blocks = lam.reshape(n_blocks, block)

        def one_block(carry, pieces):
            load_acc, soft_acc = carry
            cols, qn, lam_b, wt_b = pieces
            dots = lax.dot_general(
                fac_coords, cols, (((1,), (1,)), ((), ())), preferred_element_type=jnp.float32
            )
            cost = (pnorm[:, None] + qn[None, :] - 2.0 * dots) / width
            zval = (lam_b[None, :] - cost - mu[:, None] * wt_b[None, :]) / tau
            share = opened[:, None] * jax.nn.sigmoid(zval)
            load_acc = load_acc + grouped_sum(share * wt_b[None, :])
            soft_acc = soft_acc + grouped_sum(jax.nn.softplus(zval) * wt_b[None, :])
            return ((load_acc, soft_acc), jnp.sum(share, axis=0))

        zeros_rows = jnp.zeros((n_rows,), jnp.float32)
        carry, cover_parts = lax.scan(
            one_block,
            (zeros_rows, zeros_rows),
            (coord_blocks, qnorm_blocks, lam_blocks, weight_blocks),
        )
        cover_part = cover_parts.reshape(n_cols)
        soft_part = -tau * opened * carry[1]
        lam_local = grouped_sum(weight * lam)
        facility_local = opened * fixed_cost - mu * capacity
        load, soft, lam_total = together((carry[0], soft_part, lam_local), "cust")
        row_total = grouped_sum(facility_local + soft)
        cover, row_sum = together((cover_part, row_total), FAC)
        new_lam = lam + size * weight * (1.0 - cover) / (1.0 + cover)
        bound = (row_sum + lam_total) / total_cust
        bound_list.append(bound)
        lam = new_lam
        mu = jnp.maximum(0.0, mu + size * (load - capacity) / (load + capacity))
    return (lam, mu, jnp.stack(bound_list))


def solution(mesh):
    finer = Mesh(mesh.devices.reshape(4, 8, mesh.shape["cust"]), ("fac_0", "fac_1", "cust"))
    return jax.shard_map(
        local,
        mesh=finer,
        in_specs=(
            P(FAC, None),
            P(CUST_FAC, None),
            P(FAC),
            P("cust"),
            P(FAC),
            P(FAC),
            P(FAC),
            P("cust"),
        ),
        out_specs=(P("cust"), P(FAC), P()),
        check_vma=False,
    )
```

profile of v0, /device:TPU:1, one launch (start us, length us, event | category | flops | bytes accessed | tf_op | source)
XLA Modules:
  0.0 478.1 jit_solution(1039596463177208030)
XLA Ops:
  7.2 13.3 %all-gather = bf16[2048,128]{1,0:T(8,128)(2,1)} all-gather(bf16[512,128]{1,0:T(8,128)(2,1)} %param.15), channel_id=2, replica_groups=mesh['fac_0'=4,'fac_1'=8,'cust'=8] {'fac_0'}, dimensions={0}, use_global_device_ids=true | all-gather | bytes 655360 | tf_op jit(solution)/shard_map/all_gather | solution.py:23
  23.0 1.5 multiply_reduce_fusion.7
  25.5 53.8 %all-gather.4.cloned.1.call-done = bf16[32,512,128]{2,1,0:T(8,128)(2,1)} async-done(((bf16[4,512,128]{2,1,0:T(8,128)(2,1)}), bf16[32,512,128]{2,1,0:T(8,128)(2,1)}) %all-gather.4.cloned.1.call-update) | async-done | bytes 4194320 | tf_op jit(solution)/shard_map/all_gather | solution.py:23
  79.3 4.7 copy.18
  84.0 2.3 multiply_reduce_fusion.3
  86.4 54.9 %while.45 = (s32[]{:T(128)}, f32[512]{0:T(512)S(1)}, f32[512]{0:T(512)S(1)}, f32[8,2048]{1,0:T(8,128)S(1)}, f32[512]{0:T(512)S(1)}, /*index=5*/f32[8,2048]{1,0:T...) while((s32[]{:T(128)}, f32[512]{0:T(512)S(1)}, ...), condition=%wide.region_6.7_spmd.clone, body=%wide.region_2.6_spmd.clone.sunk | while | flops 292551680 | bytes 776863 | solution.py:96
  86.5 6.6 %fusion.43 = (f32[512]{0:T(512)S(1)}, f32[512]{0:T(512)S(1)}, f32[2048]{0:T(1024)S(1)}) fusion(f32[2048]{0:T(1024)S(1)} %bitcast.126, f32[512]{0:T(512)S(1)} %get-tuple-element.699, f32[512]{0:T(512)S(1)} %get-tuple-element.705, bf16[512,128]{1,0:T(8,128)(2,1)S(1)} %get-tuple-element.704, bf16[8,2048,128]{2,1,0:T(8,128)(2,1)} %get-tuple-element.703, ...), kind=kOutput, calls=%fused_computation.2.clone.1 | convolution fusion | flops 292549632 | bytes 698880 | tf_op jit(solution)/shard_map/while/body/eval_jaxpr/dot_general | solution.py:85
  93.4 6.5 %fusion.43 = (f32[512]{0:T(512)S(1)}, f32[512]{0:T(512)S(1)}, f32[2048]{0:T(1024)S(1)}) fusion(f32[2048]{0:T(1024)S(1)} %bitcast.126, f32[512]{0:T(512)S(1)} %get-tuple-element.699, f32[512]{0:T(512)S(1)} %get-tuple-element.705, bf16[512,128]{1,0:T(8,128)(2,1)S(1)} %get-tuple-element.704, bf16[8,2048,128]{2,1,0:T(8,128)(2,1)} %get-tuple-element.703, ...), kind=kOutput, calls=%fused_computation.2.clone.1 | convolution fusion | flops 292549632 | bytes 698880 | tf_op jit(solution)/shard_map/while/body/eval_jaxpr/dot_general | solution.py:85
  100.3 6.5 %fusion.43 = (f32[512]{0:T(512)S(1)}, f32[512]{0:T(512)S(1)}, f32[2048]{0:T(1024)S(1)}) fusion(f32[2048]{0:T(1024)S(1)} %bitcast.126, f32[512]{0:T(512)S(1)} %get-tuple-element.699, f32[512]{0:T(512)S(1)} %get-tuple-element.705, bf16[512,128]{1,0:T(8,128)(2,1)S(1)} %get-tuple-element.704, bf16[8,2048,128]{2,1,0:T(8,128)(2,1)} %get-tuple-element.703, ...), kind=kOutput, calls=%fused_computation.2.clone.1 | convolution fusion | flops 292549632 | bytes 698880 | tf_op jit(solution)/shard_map/while/body/eval_jaxpr/dot_general | solution.py:85
  107.1 6.5 %fusion.43 = (f32[512]{0:T(512)S(1)}, f32[512]{0:T(512)S(1)}, f32[2048]{0:T(1024)S(1)}) fusion(f32[2048]{0:T(1024)S(1)} %bitcast.126, f32[512]{0:T(512)S(1)} %get-tuple-element.699, f32[512]{0:T(512)S(1)} %get-tuple-element.705, bf16[512,128]{1,0:T(8,128)(2,1)S(1)} %get-tuple-element.704, bf16[8,2048,128]{2,1,0:T(8,128)(2,1)} %get-tuple-element.703, ...), kind=kOutput, calls=%fused_computation.2.clone.1 | convolution fusion | flops 292549632 | bytes 698880 | tf_op jit(solution)/shard_map/while/body/eval_jaxpr/dot_general | solution.py:85
  114.0 6.5 %fusion.43 = (f32[512]{0:T(512)S(1)}, f32[512]{0:T(512)S(1)}, f32[2048]{0:T(1024)S(1)}) fusion(f32[2048]{0:T(1024)S(1)} %bitcast.126, f32[512]{0:T(512)S(1)} %get-tuple-element.699, f32[512]{0:T(512)S(1)} %get-tuple-element.705, bf16[512,128]{1,0:T(8,128)(2,1)S(1)} %get-tuple-element.704, bf16[8,2048,128]{2,1,0:T(8,128)(2,1)} %get-tuple-element.703, ...), kind=kOutput, calls=%fused_computation.2.clone.1 | convolution fusion | flops 292549632 | bytes 698880 | tf_op jit(solution)/shard_map/while/body/eval_jaxpr/dot_general | solution.py:85
  120.8 6.5 %fusion.43 = (f32[512]{0:T(512)S(1)}, f32[512]{0:T(512)S(1)}, f32[2048]{0:T(1024)S(1)}) fusion(f32[2048]{0:T(1024)S(1)} %bitcast.126, f32[512]{0:T(512)S(1)} %get-tuple-element.699, f32[512]{0:T(512)S(1)} %get-tuple-element.705, bf16[512,128]{1,0:T(8,128)(2,1)S(1)} %get-tuple-element.704, bf16[8,2048,128]{2,1,0:T(8,128)(2,1)} %get-tuple-element.703, ...), kind=kOutput, calls=%fused_computation.2.clone.1 | convolution fusion | flops 292549632 | bytes 698880 | tf_op jit(solution)/shard_map/while/body/eval_jaxpr/dot_general | solution.py:85
  127.7 6.5 %fusion.43 = (f32[512]{0:T(512)S(1)}, f32[512]{0:T(512)S(1)}, f32[2048]{0:T(1024)S(1)}) fusion(f32[2048]{0:T(1024)S(1)} %bitcast.126, f32[512]{0:T(512)S(1)} %get-tuple-element.699, f32[512]{0:T(512)S(1)} %get-tuple-element.705, bf16[512,128]{1,0:T(8,128)(2,1)S(1)} %get-tuple-element.704, bf16[8,2048,128]{2,1,0:T(8,128)(2,1)} %get-tuple-element.703, ...), kind=kOutput, calls=%fused_computation.2.clone.1 | convolution fusion | flops 292549632 | bytes 698880 | tf_op jit(solution)/shard_map/while/body/eval_jaxpr/dot_general | solution.py:85
  134.6 6.5 %fusion.43 = (f32[512]{0:T(512)S(1)}, f32[512]{0:T(512)S(1)}, f32[2048]{0:T(1024)S(1)}) fusion(f32[2048]{0:T(1024)S(1)} %bitcast.126, f32[512]{0:T(512)S(1)} %get-tuple-element.699, f32[512]{0:T(512)S(1)} %get-tuple-element.705, bf16[512,128]{1,0:T(8,128)(2,1)S(1)} %get-tuple-element.704, bf16[8,2048,128]{2,1,0:T(8,128)(2,1)} %get-tuple-element.703, ...), kind=kOutput, calls=%fused_computation.2.clone.1 | convolution fusion | flops 292549632 | bytes 698880 | tf_op jit(solution)/shard_map/while/body/eval_jaxpr/dot_general | solution.py:85
  142.7 5.1 %all-to-all-start = ((f32[8,1,1025]{2,1,0:T(1,128)}), f32[8,1,1025]{2,1,0:T(1,128)S(1)}, u32[]{:S(2)}, u32[]{:S(2)}) async-start(f32[8,1,1025]{2,1,0:T(1,128)} %broadcast_in_dim.30), calls=%async_computation | async-start | bytes 73728 | tf_op jit(solution)/shard_map/all_to_all | solution.py:36
  147.8 4.7 all-to-all-done
  153.9 2.4 broadcast_in_dim.31
  156.3 7.1 %all-to-all-start.1 = ((f32[32,1,16385]{2,1,0:T(1,128)}), f32[32,1,16385]{2,1,0:T(1,128)S(1)}, u32[]{:S(2)}, u32[]{:S(2)}) async-start(f32[32,1,16385]{2,1,0:T(1,128)} %broadcast_in_dim.31), calls=%async_computation.1 | async-start | bytes 4227072 | tf_op jit(solution)/shard_map/all_to_all | solution.py:36
  163.4 49.0 %all-to-all-done.1 = f32[32,1,16385]{2,1,0:T(1,128)S(1)} async-done(((f32[32,1,16385]{2,1,0:T(1,128)}), f32[32,1,16385]{2,1,0:T(1,128)S(1)}, u32[]{:S(2)}, u32[]{:S(2)}) %all-to-all-start.1) | async-done | bytes 2097312 | tf_op jit(solution)/shard_map/all_to_all | solution.py:36
  214.2 54.9 %while.46 = (s32[]{:T(128)}, f32[512]{0:T(512)S(1)}, f32[512]{0:T(512)S(1)}, f32[8,2048]{1,0:T(8,128)S(1)}, f32[512]{0:T(512)S(1)}, /*index=5*/f32[8,2048]{1,0:T...) while((s32[]{:T(128)}, f32[512]{0:T(512)S(1)}, ...), condition=%wide.region_15.16_spmd.clone, body=%wide.region_11.15_spmd.clone.sunk | while | flops 292551680 | bytes 776863 | solution.py:96
  214.3 6.5 %fusion.45 = (f32[512]{0:T(512)S(1)}, f32[512]{0:T(512)S(1)}, f32[2048]{0:T(1024)S(1)}) fusion(f32[2048]{0:T(1024)S(1)} %bitcast.129, f32[512]{0:T(512)S(1)} %get-tuple-element.741, f32[512]{0:T(512)S(1)} %get-tuple-element.747, bf16[512,128]{1,0:T(8,128)(2,1)S(1)} %get-tuple-element.746, bf16[8,2048,128]{2,1,0:T(8,128)(2,1)} %get-tuple-element.745, ...), kind=kOutput, calls=%fused_computation.21.clone.1 | convolution fusion | flops 292549632 | bytes 698880 | tf_op jit(solution)/shard_map/while/body/eval_jaxpr/dot_general | solution.py:85
  221.2 6.6 %fusion.45 = (f32[512]{0:T(512)S(1)}, f32[512]{0:T(512)S(1)}, f32[2048]{0:T(1024)S(1)}) fusion(f32[2048]{0:T(1024)S(1)} %bitcast.129, f32[512]{0:T(512)S(1)} %get-tuple-element.741, f32[512]{0:T(512)S(1)} %get-tuple-element.747, bf16[512,128]{1,0:T(8,128)(2,1)S(1)} %get-tuple-element.746, bf16[8,2048,128]{2,1,0:T(8,128)(2,1)} %get-tuple-element.745, ...), kind=kOutput, calls=%fused_computation.21.clone.1 | convolution fusion | flops 292549632 | bytes 698880 | tf_op jit(solution)/shard_map/while/body/eval_jaxpr/dot_general | solution.py:85
  228.0 6.5 %fusion.45 = (f32[512]{0:T(512)S(1)}, f32[512]{0:T(512)S(1)}, f32[2048]{0:T(1024)S(1)}) fusion(f32[2048]{0:T(1024)S(1)} %bitcast.129, f32[512]{0:T(512)S(1)} %get-tuple-element.741, f32[512]{0:T(512)S(1)} %get-tuple-element.747, bf16[512,128]{1,0:T(8,128)(2,1)S(1)} %get-tuple-element.746, bf16[8,2048,128]{2,1,0:T(8,128)(2,1)} %get-tuple-element.745, ...), kind=kOutput, calls=%fused_computation.21.clone.1 | convolution fusion | flops 292549632 | bytes 698880 | tf_op jit(solution)/shard_map/while/body/eval_jaxpr/dot_general | solution.py:85
  234.9 6.5 %fusion.45 = (f32[512]{0:T(512)S(1)}, f32[512]{0:T(512)S(1)}, f32[2048]{0:T(1024)S(1)}) fusion(f32[2048]{0:T(1024)S(1)} %bitcast.129, f32[512]{0:T(512)S(1)} %get-tuple-element.741, f32[512]{0:T(512)S(1)} %get-tuple-element.747, bf16[512,128]{1,0:T(8,128)(2,1)S(1)} %get-tuple-element.746, bf16[8,2048,128]{2,1,0:T(8,128)(2,1)} %get-tuple-element.745, ...), kind=kOutput, calls=%fused_computation.21.clone.1 | convolution fusion | flops 292549632 | bytes 698880 | tf_op jit(solution)/shard_map/while/body/eval_jaxpr/dot_general | solution.py:85
  241.7 6.5 %fusion.45 = (f32[512]{0:T(512)S(1)}, f32[512]{0:T(512)S(1)}, f32[2048]{0:T(1024)S(1)}) fusion(f32[2048]{0:T(1024)S(1)} %bitcast.129, f32[512]{0:T(512)S(1)} %get-tuple-element.741, f32[512]{0:T(512)S(1)} %get-tuple-element.747, bf16[512,128]{1,0:T(8,128)(2,1)S(1)} %get-tuple-element.746, bf16[8,2048,128]{2,1,0:T(8,128)(2,1)} %get-tuple-element.745, ...), kind=kOutput, calls=%fused_computation.21.clone.1 | convolution fusion | flops 292549632 | bytes 698880 | tf_op jit(solution)/shard_map/while/body/eval_jaxpr/dot_general | solution.py:85
  248.6 6.6 %fusion.45 = (f32[512]{0:T(512)S(1)}, f32[512]{0:T(512)S(1)}, f32[2048]{0:T(1024)S(1)}) fusion(f32[2048]{0:T(1024)S(1)} %bitcast.129, f32[512]{0:T(512)S(1)} %get-tuple-element.741, f32[512]{0:T(512)S(1)} %get-tuple-element.747, bf16[512,128]{1,0:T(8,128)(2,1)S(1)} %get-tuple-element.746, bf16[8,2048,128]{2,1,0:T(8,128)(2,1)} %get-tuple-element.745, ...), kind=kOutput, calls=%fused_computation.21.clone.1 | convolution fusion | flops 292549632 | bytes 698880 | tf_op jit(solution)/shard_map/while/body/eval_jaxpr/dot_general | solution.py:85
  255.5 6.5 %fusion.45 = (f32[512]{0:T(512)S(1)}, f32[512]{0:T(512)S(1)}, f32[2048]{0:T(1024)S(1)}) fusion(f32[2048]{0:T(1024)S(1)} %bitcast.129, f32[512]{0:T(512)S(1)} %get-tuple-element.741, f32[512]{0:T(512)S(1)} %get-tuple-element.747, bf16[512,128]{1,0:T(8,128)(2,1)S(1)} %get-tuple-element.746, bf16[8,2048,128]{2,1,0:T(8,128)(2,1)} %get-tuple-element.745, ...), kind=kOutput, calls=%fused_computation.21.clone.1 | convolution fusion | flops 292549632 | bytes 698880 | tf_op jit(solution)/shard_map/while/body/eval_jaxpr/dot_general | solution.py:85
  262.3 6.5 %fusion.45 = (f32[512]{0:T(512)S(1)}, f32[512]{0:T(512)S(1)}, f32[2048]{0:T(1024)S(1)}) fusion(f32[2048]{0:T(1024)S(1)} %bitcast.129, f32[512]{0:T(512)S(1)} %get-tuple-element.741, f32[512]{0:T(512)S(1)} %get-tuple-element.747, bf16[512,128]{1,0:T(8,128)(2,1)S(1)} %get-tuple-element.746, bf16[8,2048,128]{2,1,0:T(8,128)(2,1)} %get-tuple-element.745, ...), kind=kOutput, calls=%fused_computation.21.clone.1 | convolution fusion | flops 292549632 | bytes 698880 | tf_op jit(solution)/shard_map/while/body/eval_jaxpr/dot_general | solution.py:85
  270.4 5.4 %all-to-all-start.2 = ((f32[8,1,1025]{2,1,0:T(1,128)}), f32[8,1,1025]{2,1,0:T(1,128)S(1)}, u32[]{:S(2)}, u32[]{:S(2)}) async-start(f32[8,1,1025]{2,1,0:T(1,128)} %broadcast_in_dim.32), calls=%async_computation.2 | async-start | bytes 73728 | tf_op jit(solution)/shard_map/all_to_all | solution.py:36
  275.9 4.7 all-to-all-done.2
  281.9 2.4 broadcast_in_dim.33
  284.3 5.9 %all-to-all-start.3 = ((f32[32,1,16385]{2,1,0:T(1,128)}), f32[32,1,16385]{2,1,0:T(1,128)S(1)}, u32[]{:S(2)}, u32[]{:S(2)}) async-start(f32[32,1,16385]{2,1,0:T(1,128)} %broadcast_in_dim.33), calls=%async_computation.3 | async-start | bytes 4227072 | tf_op jit(solution)/shard_map/all_to_all | solution.py:36
  290.2 49.1 %all-to-all-done.3 = f32[32,1,16385]{2,1,0:T(1,128)S(1)} async-done(((f32[32,1,16385]{2,1,0:T(1,128)}), f32[32,1,16385]{2,1,0:T(1,128)S(1)}, u32[]{:S(2)}, u32[]{:S(2)}) %all-to-all-start.3) | async-done | bytes 2097312 | tf_op jit(solution)/shard_map/all_to_all | solution.py:36
  339.4 1.2 reduce_sum.232
  341.2 54.9 %while.47 = (s32[]{:T(128)}, f32[512]{0:T(512)S(1)}, f32[512]{0:T(512)S(1)}, f32[8,2048]{1,0:T(8,128)S(1)}, f32[512]{0:T(512)S(1)}, /*index=5*/f32[8,2048]{1,0:T...) while((s32[]{:T(128)}, f32[512]{0:T(512)S(1)}, ...), condition=%wide.region_24.25_spmd.clone, body=%wide.region_20.0_spmd.clone.sunk | while | flops 292551680 | bytes 776863 | solution.py:96
  341.3 6.6 %fusion.47 = (f32[512]{0:T(512)S(1)}, f32[512]{0:T(512)S(1)}, f32[2048]{0:T(1024)S(1)}) fusion(f32[2048]{0:T(1024)S(1)} %bitcast.132, f32[512]{0:T(512)S(1)} %get-tuple-element.783, f32[512]{0:T(512)S(1)} %get-tuple-element.789, bf16[512,128]{1,0:T(8,128)(2,1)S(1)} %get-tuple-element.788, bf16[8,2048,128]{2,1,0:T(8,128)(2,1)} %get-tuple-element.787, ...), kind=kOutput, calls=%fused_computation.40.clone.1 | convolution fusion | flops 292549632 | bytes 698880 | tf_op jit(solution)/shard_map/while/body/eval_jaxpr/dot_general | solution.py:85
  348.2 6.5 %fusion.47 = (f32[512]{0:T(512)S(1)}, f32[512]{0:T(512)S(1)}, f32[2048]{0:T(1024)S(1)}) fusion(f32[2048]{0:T(1024)S(1)} %bitcast.132, f32[512]{0:T(512)S(1)} %get-tuple-element.783, f32[512]{0:T(512)S(1)} %get-tuple-element.789, bf16[512,128]{1,0:T(8,128)(2,1)S(1)} %get-tuple-element.788, bf16[8,2048,128]{2,1,0:T(8,128)(2,1)} %get-tuple-element.787, ...), kind=kOutput, calls=%fused_computation.40.clone.1 | convolution fusion | flops 292549632 | bytes 698880 | tf_op jit(solution)/shard_map/while/body/eval_jaxpr/dot_general | solution.py:85
  355.0 6.5 %fusion.47 = (f32[512]{0:T(512)S(1)}, f32[512]{0:T(512)S(1)}, f32[2048]{0:T(1024)S(1)}) fusion(f32[2048]{0:T(1024)S(1)} %bitcast.132, f32[512]{0:T(512)S(1)} %get-tuple-element.783, f32[512]{0:T(512)S(1)} %get-tuple-element.789, bf16[512,128]{1,0:T(8,128)(2,1)S(1)} %get-tuple-element.788, bf16[8,2048,128]{2,1,0:T(8,128)(2,1)} %get-tuple-element.787, ...), kind=kOutput, calls=%fused_computation.40.clone.1 | convolution fusion | flops 292549632 | bytes 698880 | tf_op jit(solution)/shard_map/while/body/eval_jaxpr/dot_general | solution.py:85
  361.9 6.5 %fusion.47 = (f32[512]{0:T(512)S(1)}, f32[512]{0:T(512)S(1)}, f32[2048]{0:T(1024)S(1)}) fusion(f32[2048]{0:T(1024)S(1)} %bitcast.132, f32[512]{0:T(512)S(1)} %get-tuple-element.783, f32[512]{0:T(512)S(1)} %get-tuple-element.789, bf16[512,128]{1,0:T(8,128)(2,1)S(1)} %get-tuple-element.788, bf16[8,2048,128]{2,1,0:T(8,128)(2,1)} %get-tuple-element.787, ...), kind=kOutput, calls=%fused_computation.40.clone.1 | convolution fusion | flops 292549632 | bytes 698880 | tf_op jit(solution)/shard_map/while/body/eval_jaxpr/dot_general | solution.py:85
  368.8 6.5 %fusion.47 = (f32[512]{0:T(512)S(1)}, f32[512]{0:T(512)S(1)}, f32[2048]{0:T(1024)S(1)}) fusion(f32[2048]{0:T(1024)S(1)} %bitcast.132, f32[512]{0:T(512)S(1)} %get-tuple-element.783, f32[512]{0:T(512)S(1)} %get-tuple-element.789, bf16[512,128]{1,0:T(8,128)(2,1)S(1)} %get-tuple-element.788, bf16[8,2048,128]{2,1,0:T(8,128)(2,1)} %get-tuple-element.787, ...), kind=kOutput, calls=%fused_computation.40.clone.1 | convolution fusion | flops 292549632 | bytes 698880 | tf_op jit(solution)/shard_map/while/body/eval_jaxpr/dot_general | solution.py:85
  375.6 6.5 %fusion.47 = (f32[512]{0:T(512)S(1)}, f32[512]{0:T(512)S(1)}, f32[2048]{0:T(1024)S(1)}) fusion(f32[2048]{0:T(1024)S(1)} %bitcast.132, f32[512]{0:T(512)S(1)} %get-tuple-element.783, f32[512]{0:T(512)S(1)} %get-tuple-element.789, bf16[512,128]{1,0:T(8,128)(2,1)S(1)} %get-tuple-element.788, bf16[8,2048,128]{2,1,0:T(8,128)(2,1)} %get-tuple-element.787, ...), kind=kOutput, calls=%fused_computation.40.clone.1 | convolution fusion | flops 292549632 | bytes 698880 | tf_op jit(solution)/shard_map/while/body/eval_jaxpr/dot_general | solution.py:85
  382.5 6.5 %fusion.47 = (f32[512]{0:T(512)S(1)}, f32[512]{0:T(512)S(1)}, f32[2048]{0:T(1024)S(1)}) fusion(f32[2048]{0:T(1024)S(1)} %bitcast.132, f32[512]{0:T(512)S(1)} %get-tuple-element.783, f32[512]{0:T(512)S(1)} %get-tuple-element.789, bf16[512,128]{1,0:T(8,128)(2,1)S(1)} %get-tuple-element.788, bf16[8,2048,128]{2,1,0:T(8,128)(2,1)} %get-tuple-element.787, ...), kind=kOutput, calls=%fused_computation.40.clone.1 | convolution fusion | flops 292549632 | bytes 698880 | tf_op jit(solution)/shard_map/while/body/eval_jaxpr/dot_general | solution.py:85
  389.4 6.5 %fusion.47 = (f32[512]{0:T(512)S(1)}, f32[512]{0:T(512)S(1)}, f32[2048]{0:T(1024)S(1)}) fusion(f32[2048]{0:T(1024)S(1)} %bitcast.132, f32[512]{0:T(512)S(1)} %get-tuple-element.783, f32[512]{0:T(512)S(1)} %get-tuple-element.789, bf16[512,128]{1,0:T(8,128)(2,1)S(1)} %get-tuple-element.788, bf16[8,2048,128]{2,1,0:T(8,128)(2,1)} %get-tuple-element.787, ...), kind=kOutput, calls=%fused_computation.40.clone.1 | convolution fusion | flops 292549632 | bytes 698880 | tf_op jit(solution)/shard_map/while/body/eval_jaxpr/dot_general | solution.py:85
  397.5 5.4 %all-to-all-start.4 = ((f32[8,1,1025]{2,1,0:T(1,128)}), f32[8,1,1025]{2,1,0:T(1,128)S(1)}, u32[]{:S(2)}, u32[]{:S(2)}) async-start(f32[8,1,1025]{2,1,0:T(1,128)} %broadcast_in_dim.42), calls=%async_computation.4 | async-start | bytes 73728 | tf_op jit(solution)/shard_map/all_to_all | solution.py:36
  402.9 4.7 all-to-all-done.4
  409.5 2.4 broadcast_in_dim.43
  412.0 5.9 %all-to-all-start.5 = ((f32[32,1,16385]{2,1,0:T(1,128)}), f32[32,1,16385]{2,1,0:T(1,128)S(1)}, u32[]{:S(2)}, u32[]{:S(2)}) async-start(f32[32,1,16385]{2,1,0:T(1,128)} %broadcast_in_dim.43), calls=%async_computation.5 | async-start | bytes 4227072 | tf_op jit(solution)/shard_map/all_to_all | solution.py:36
  423.0 44.0 %all-to-all-done.5 = f32[32,1,16385]{2,1,0:T(1,128)S(1)} async-done(((f32[32,1,16385]{2,1,0:T(1,128)}), f32[32,1,16385]{2,1,0:T(1,128)S(1)}, u32[]{:S(2)}, u32[]{:S(2)}) %all-to-all-start.5) | async-done | bytes 2097312 | tf_op jit(solution)/shard_map/all_to_all | solution.py:36
  (189 shorter events, 26.2 us)
Async XLA Ops:
  7.2 72.2 %all-gather.4.cloned.1.call-start = ((), (), s32[]{:S(2)}) async-start(), calls=%async_computation.6 | async-start | bytes 4718592 | tf_op jit(solution)/shard_map/all_gather | solution.py:23
  79.3 4.7 copy-start
  84.0 2.4 copy-start.3
  84.0 2.4 copy-start.7
  86.4 55.0 %copy-start.4 = (s32[512]{0:T(512)S(1)}, s32[512]{0:T(512)}, u32[]{:S(2)}) copy-start(s32[512]{0:T(512)} %param.16) | copy-start | bytes 6148
  86.4 66.1 %copy-start.5 = (f32[512]{0:T(512)S(1)}, f32[512]{0:T(512)}, u32[]{:S(2)}) copy-start(f32[512]{0:T(512)} %param.19) | copy-start | bytes 6148
  86.4 66.1 %copy-start.6 = (f32[512]{0:T(512)S(1)}, f32[512]{0:T(512)}, u32[]{:S(2)}) copy-start(f32[512]{0:T(512)} %param.18) | copy-start | bytes 6148
  142.7 9.8 %all-to-all-start = ((f32[8,1,1025]{2,1,0:T(1,128)}), f32[8,1,1025]{2,1,0:T(1,128)S(1)}, u32[]{:S(2)}, u32[]{:S(2)}) async-start(f32[8,1,1025]{2,1,0:T(1,128)} %broadcast_in_dim.30), calls=%async_computation | async-start | bytes 73728 | tf_op jit(solution)/shard_map/all_to_all | solution.py:36
  153.8 59.7 %copy-start.1 = (s32[16384]{0:T(1024)S(1)}, s32[16384]{0:T(1024)}, u32[]{:S(2)}) copy-start(s32[16384]{0:T(1024)} %param.17) | copy-start | bytes 196612
  153.9 59.7 %copy-start.2 = (f32[16384]{0:T(1024)S(1)}, f32[16384]{0:T(1024)}, u32[]{:S(2)}) copy-start(f32[16384]{0:T(1024)} %param.21) | copy-start | bytes 196612
  156.3 56.0 %all-to-all-start.1 = ((f32[32,1,16385]{2,1,0:T(1,128)}), f32[32,1,16385]{2,1,0:T(1,128)S(1)}, u32[]{:S(2)}, u32[]{:S(2)}) async-start(f32[32,1,16385]{2,1,0:T(1,128)} %broadcast_in_dim.31), calls=%async_computation.1 | async-start | bytes 4227072 | tf_op jit(solution)/shard_map/all_to_all | solution.py:36
  270.4 10.2 %all-to-all-start.2 = ((f32[8,1,1025]{2,1,0:T(1,128)}), f32[8,1,1025]{2,1,0:T(1,128)S(1)}, u32[]{:S(2)}, u32[]{:S(2)}) async-start(f32[8,1,1025]{2,1,0:T(1,128)} %broadcast_in_dim.32), calls=%async_computation.2 | async-start | bytes 73728 | tf_op jit(solution)/shard_map/all_to_all | solution.py:36
  284.3 55.0 %all-to-all-start.3 = ((f32[32,1,16385]{2,1,0:T(1,128)}), f32[32,1,16385]{2,1,0:T(1,128)S(1)}, u32[]{:S(2)}, u32[]{:S(2)}) async-start(f32[32,1,16385]{2,1,0:T(1,128)} %broadcast_in_dim.33), calls=%async_computation.3 | async-start | bytes 4227072 | tf_op jit(solution)/shard_map/all_to_all | solution.py:36
  397.5 10.2 %all-to-all-start.4 = ((f32[8,1,1025]{2,1,0:T(1,128)}), f32[8,1,1025]{2,1,0:T(1,128)S(1)}, u32[]{:S(2)}, u32[]{:S(2)}) async-start(f32[8,1,1025]{2,1,0:T(1,128)} %broadcast_in_dim.42), calls=%async_computation.4 | async-start | bytes 73728 | tf_op jit(solution)/shard_map/all_to_all | solution.py:36
  412.0 55.0 %all-to-all-start.5 = ((f32[32,1,16385]{2,1,0:T(1,128)}), f32[32,1,16385]{2,1,0:T(1,128)S(1)}, u32[]{:S(2)}, u32[]{:S(2)}) async-start(f32[32,1,16385]{2,1,0:T(1,128)} %broadcast_in_dim.43), calls=%async_computation.5 | async-start | bytes 4227072 | tf_op jit(solution)/shard_map/all_to_all | solution.py:36
Sparse Core Ops, SparseCore 0:
  20.6 58.6 all-gather.3
where the time goes:
time: 479 us; the launch traced here: 478 us
  waiting for transfers between devices  210 us (44%)
  matrix products  157 us (33%)
  starting transfers between devices  34.8 us (7%)
  local copies, waits for them, and re-layouts  23.9 us (5%)
  other arithmetic  19.2 us (4%)
  between operations  18.2 us (4%)
  blocking collectives  13.3 us (3%)
    dot_general x24, matrix products, one_block(): lax.dot_general(fac_coords, cols, (((1,), (1,)), ((), ())), preferred_ele...  157 us
    all_to_all x6, waiting for transfers between devices, copy_for_each(): lax.all_to_all(jnp.broadcast_to(x[None], (size, *x.shape)), axis, 0, 0, t...  156 us
    all_gather x1, waiting for transfers between devices, stacked_from(): blocks = lax.all_gather(blocks, axes[k])  53.8 us
    all_to_all x6, starting transfers between devices, copy_for_each(): lax.all_to_all(jnp.broadcast_to(x[None], (size, *x.shape)), axis, 0, 0, t...  34.7 us
    all_gather x1, blocking collectives, stacked_from(): blocks = lax.all_gather(blocks, axes[k])  13.3 us
  transfers between devices with their start and end apart: 7, of which 7 were waited for; matrix products, arithmetic and copies ran while one was open for 2% of the time, Pallas kernels for 0%

commit v1 on v0

v1 whole, which is shorter than its diff:
```python
import functools
import math

import jax
import jax.numpy as jnp
from jax import lax
from jax.experimental import pallas as pl
from jax.experimental.pallas import tpu as pltpu
from jax.sharding import PartitionSpec as P

ITERS = 3
CORES = 2
TAU = 0.1
BIG = float(2**20)
LN2 = math.log(2.0)
MESH = pl.DeviceIdType.MESH
F32 = jnp.float32
BF16 = jnp.bfloat16


def split3(v):
    hi = v.astype(BF16).astype(F32)
    rest = v - hi
    mid = rest.astype(BF16).astype(F32)
    lo = (rest - mid).astype(BF16).astype(F32)
    return hi, mid, lo


def place_rows(shape, rows):
    at = lax.broadcasted_iota(jnp.int32, shape, 0)
    out = jnp.zeros(shape, F32)
    for index, row in rows.items():
        out = jnp.where(at == index, jnp.broadcast_to(row, shape), out)
    return out


def fold(v):
    total = v[:, :128]
    for j in range(1, v.shape[1] // 128):
        total = total + v[:, 128 * j : 128 * (j + 1)]
    return total


def kernel(
    ny, nz, nx,
    fac_ref, cust_ref, flag_ref, dem_ref, fix_ref, cap_ref, mu_ref, lam_ref,
    lam_out, mu_out, bound_out,
    fp, fx, r, fv, d8, s0, s1, ld, cv, lg, lam_s, mu_s, pn_s, cap_s, tt,
    cx, l1, l2, fin, tf,
    fp_send, fp_recv, fv_send, fv_recv, r_send, r_recv, fw_send,
    c_send, c_recv, l1_send, l1_recv, l2_send, l2_recv, fin_send, fin_recv, tf_send, tf_recv,
):
    ng = ny * CORES
    half = fac_ref.shape[0] // CORES
    cols = cust_ref.shape[0]
    width = fac_ref.shape[1]
    hrows = half // 128
    crows = cols // 128
    total_cust = float(dem_ref.shape[0] * 128 * nx * CORES)
    f = lax.axis_index("fac")
    c = lax.axis_index("cust")
    y, z = f // nz, f % nz
    x, core = c // CORES, c % CORES
    g = y * CORES + core
    scale = math.log2(math.e) / (width * TAU)

    def at(y_, z_, x_, core_):
        return (y_ * nz + z_, x_ * CORES + core_)

    def z_dev(o):
        zp = (z + o) % nz
        return zp, at(y, zp, x, core)

    def g_dev(o):
        gp = (g + o) % ng
        return gp, at(gp // CORES, z, x, gp % CORES)

    def x_dev(o):
        xp = (x + o) % nx
        return xp, at(y, z, xp, core)

    def near(o, n):
        step = (o + 1) // 2
        return (step * (2 * (o % 2) - 1) + n) % n

    def remote(src, dst, send, recv, dev):
        return pltpu.make_async_remote_copy(
            src_ref=src, dst_ref=dst, send_sem=send, recv_sem=recv, device_id=dev, device_id_type=MESH
        )

    def loop(n, body, start=0):
        lax.fori_loop(start, n, lambda i, _: (body(i), 0)[1], 0)

    barrier = pltpu.get_barrier_semaphore()

    def greet(dev_of, n):
        def body(o):
            pl.semaphore_signal(barrier, inc=1, device_id=dev_of(o)[1], device_id_type=MESH)

        loop(n, body, 1)

    greet(z_dev, nz)
    greet(g_dev, ng)
    greet(x_dev, nx)

    for j in range(crows):
        lanes = slice(128 * j, 128 * (j + 1))
        qt = cust_ref[128 * j : 128 * (j + 1), :].astype(F32).T
        r[g, 0:width, lanes] = (2.0 * qt).astype(BF16)
        qn = jnp.sum(qt * qt, axis=0, keepdims=True)
        dem = dem_ref[pl.ds(f * crows + j, 1), :].astype(F32)
        lam0 = lam_ref[pl.ds(f * crows + j, 1), :]
        qh, qm, ql = split3(-qn)
        one = jnp.ones((1, 128), F32)
        r[g, width : width + 16, lanes] = place_rows(
            (16, 128), {0: qh, 1: qm, 2: ql, 3: -one, 4: -one, 5: -one, 6: -dem, 7: -dem, 8: -dem}
        ).astype(BF16)
        lh, lm, ll = split3(width * lam0)
        r[g, width + 16 : width + 32, lanes] = place_rows((16, 128), {0: lh, 1: lm, 2: ll}).astype(BF16)

    mine = pl.ds(pl.multiple_of(core * half, half), half)
    opened = (flag_ref[pl.ds(core * hrows, hrows), :]).astype(F32)
    for j in range(hrows):
        pt = fac_ref[pl.ds(pl.multiple_of(core * half + 128 * j, 128), 128), :].astype(F32).T
        pn = jnp.sum(pt * pt, axis=0, keepdims=True)
        fv[z, j : j + 1, :] = pn + BIG * (1.0 - opened[j : j + 1])
    fv[z, hrows : 2 * hrows, :] = mu_ref[pl.ds(core * hrows, hrows), :]
    fv[z, 2 * hrows : 3 * hrows, :] = cap_ref[pl.ds(core * hrows, hrows), :]
    fv[z, 3 * hrows : 4 * hrows, :] = jnp.zeros((hrows, 128), F32)
    fp[z] = fac_ref[mine, :]

    pl.semaphore_wait(barrier, (nz - 1) + (ng - 1) + (nx - 1))

    chunk = pl.ds(0, width + 32)

    def fac_copy(o):
        zp, dev = z_dev(near(o, nz))
        return remote(fac_ref.at[mine], fp.at[z], fp_send.at[zp], fp_recv.at[z], dev)

    def vec_copy(o):
        zp, dev = z_dev(near(o, nz))
        return remote(fv.at[z], fv.at[z], fv_send.at[zp], fv_recv.at[z], dev)

    def own_copy(o):
        yp = (y + o) % ny
        return remote(
            r.at[g, chunk], r.at[g, chunk], r_send.at[yp * CORES + core], r_recv.at[g], at(yp, z, x, core)
        )

    def forward(yp):
        s = yp * CORES + core
        return remote(r.at[s, chunk], r.at[s, chunk], fw_send.at[yp], r_recv.at[s], at(y, z, x, 1 - core))

    loop(ny, lambda o: own_copy(o).start(), 1)
    forward(y).start()
    loop(nz, lambda o: vec_copy(o).start(), 1)
    loop(nz, lambda o: fac_copy(o).start(), 1)

    def clear(s):
        r[s, width + 32 :, :] = jnp.zeros((r.shape[1] - width - 32, cols), BF16)

    loop(ng, clear)

    def arrived(o):
        yp = (y + o) % ny
        s = yp * CORES + core
        remote(r.at[s, chunk], r.at[s, chunk], r_send.at[s], r_recv.at[s], at(y, z, x, core)).wait_recv()
        forward(yp).start()

    loop(ny, arrived, 1)

    def from_partner(yp):
        s = yp * CORES + 1 - core
        remote(r.at[s, chunk], r.at[s, chunk], fw_send.at[yp], r_recv.at[s], at(y, z, x, core)).wait_recv()

    loop(ny, from_partner)
    for s in range(ng):
        extra = r[s, width : width + 16, :].astype(F32)
        d8[s] = jnp.broadcast_to(-extra[6:7], (8, cols))
        lam = r[s, width + 16 : width + 32, :].astype(F32)
        lam_s[s : s + 1, :] = (lam[0:1] + lam[1:2] + lam[2:3]) * (1.0 / width)

    def vec_in(o):
        zp = (z + o) % nz
        remote(fv.at[zp], fv.at[zp], fv_send.at[zp], fv_recv.at[zp], at(y, z, x, core)).wait_recv()

    loop(nz, vec_in, 1)
    for zp in range(nz):
        rows = slice(hrows * zp, hrows * (zp + 1))
        pn_s[rows, :] = fv[zp, 0:hrows, :]
        mu_s[rows, :] = fv[zp, hrows : 2 * hrows, :]
        cap_s[rows, :] = fv[zp, 2 * hrows : 3 * hrows, :]

    def build_extra(b):
        for j in range(hrows):
            ph, pm, pll = split3(pn_s[pl.ds(b * hrows + j, 1), :])
            mh, mm, ml = split3(width * mu_s[pl.ds(b * hrows + j, 1), :])
            one = jnp.ones((1, 128), F32)
            top = place_rows(
                (24, 128),
                {0: one, 1: one, 2: one, 3: ph, 4: pm, 5: pll, 6: mh, 7: mm, 8: ml, 16: one, 17: one, 18: one},
            )
            block = jnp.concatenate([top, jnp.zeros((104, 128), F32)], axis=0)
            fx[b, 128 * j : 128 * (j + 1), :] = block.T.astype(BF16)

    loop(nz, build_extra)

    def fac_in(o):
        zp, _ = z_dev(near(o, nz))
        remote(fp.at[zp], fp.at[zp], fp_send.at[zp], fp_recv.at[zp], at(y, z, x, core)).wait_recv()

    loop(nz, fac_in, 1)
    loop(nz, lambda o: fac_copy(o).wait_send(), 1)
    loop(nz, lambda o: vec_copy(o).wait_send(), 1)
    loop(ny, lambda o: own_copy(o).wait_send(), 1)
    loop(ny, lambda yp: forward(yp).wait_send())

    tiles = nz * ng

    def product(slot, t):
        b, s = t // ng, t % ng
        rows = jnp.concatenate([fp[b], fx[b]], axis=1)
        slot[...] = jnp.dot(rows, r[s], preferred_element_type=F32)

    def pointwise(slot, t):
        b, s = t // ng, t % ng
        cov = cv[s]
        logs = lg[s]
        dem = d8[s]
        prod, count = None, 0
        groups = half // 8
        for i in range(groups):
            e = jnp.exp2(slot[8 * i : 8 * i + 8, :] * scale)
            u = 1.0 + e
            share = e / u
            cov = cov + share
            ld[b, 8 * i : 8 * i + 8, :] += fold(share * dem)
            prod = u if prod is None else prod * u
            count += 1
            if count == 3 or i == groups - 1:
                logs = logs + jnp.log2(prod)
                prod, count = None, 0
        cv[s] = cov
        lg[s] = logs

    def step(k):
        size = jnp.where(k == 0, 0.1, jnp.where(k == 1, 0.1 / 2, 0.1 / 3)).astype(F32)

        def zero_rows(b):
            ld[b] = jnp.zeros((half, 128), F32)

        def zero_cols(s):
            cv[s] = jnp.zeros((8, cols), F32)
            lg[s] = jnp.zeros((8, cols), F32)

        loop(nz, zero_rows)
        loop(ng, zero_cols)
        product(s0, 0)

        def two(i):
            t = 2 * i
            product(s1, t + 1)
            pointwise(s0, t)
            product(s0, lax.rem(t + 2, tiles))
            pointwise(s1, t + 1)

        loop(tiles // 2, two)

        def load_row(b):
            for j in range(hrows):
                block = ld[b, 128 * j : 128 * (j + 1), :].T
                l1[k, x, pl.ds(b * hrows + j, 1), :] = jnp.sum(block, axis=0, keepdims=True)

        loop(nz, load_row)
        soft = jnp.zeros((8, cols), F32)
        for s in range(ng):
            soft = soft + lg[s] * d8[s]
        soft = jnp.sum(fold(soft), axis=0, keepdims=True)
        priced = fold(lam_s[pl.ds(g, 1), :] * d8[g][0:1])
        own = pl.ds(z * hrows, hrows)
        rowterm = opened * fix_ref[pl.ds(core * hrows, hrows), :] - mu_s[own, :] * cap_s[own, :]
        rowterm = jnp.sum(rowterm, axis=0, keepdims=True) * (1.0 / nx)
        tt[pl.ds(k, 1), :] = priced + rowterm - (TAU * LN2) * soft
        l1[k, x, hrows * nz :, :] = tt[...]

        def l1_copy(o):
            xp, dev = x_dev(o)
            return remote(l1.at[k, x], l1.at[k, x], l1_send.at[k, xp], l1_recv.at[k, x], dev)

        loop(nx, lambda o: l1_copy(o).start(), 1)
        cx[k, g] = jnp.concatenate([jnp.sum(cv[s], axis=0, keepdims=True) for s in range(ng)], axis=0)

        def c_copy(o):
            gp, dev = g_dev(o)
            return remote(cx.at[k, g], cx.at[k, g], c_send.at[k, gp], c_recv.at[k, g], dev)

        loop(ng, lambda o: c_copy(o).start(), 1)

        def l1_in(o):
            xp, dev = x_dev(o)
            remote(l1.at[k, xp], l1.at[k, xp], l1_send.at[k, xp], l1_recv.at[k, xp], dev).wait_recv()

        loop(nx, l1_in, 1)
        part = l1[k, 0]
        for xp in range(1, nx):
            part = part + l1[k, xp]
        l2[k, z] = part

        def l2_copy(o):
            zp, dev = z_dev(near(o, nz))
            return remote(l2.at[k, z], l2.at[k, z], l2_send.at[k, zp], l2_recv.at[k, z], dev)

        loop(nz, lambda o: l2_copy(o).start(), 1)

        def c_in(o):
            gp, dev = g_dev(o)
            remote(cx.at[k, gp], cx.at[k, gp], c_send.at[k, gp], c_recv.at[k, gp], dev).wait_recv()

        loop(ng, c_in, 1)
        cover = cx[k, 0]
        for gp in range(1, ng):
            cover = cover + cx[k, gp]
        dem = jnp.concatenate([d8[s][0:1] for s in range(ng)], axis=0)
        lam_s[...] = lam_s[...] + size * dem * (1.0 - cover) / (1.0 + cover)
        for s in range(ng):
            lh, lm, ll = split3(width * lam_s[s : s + 1, :])
            r[s, width + 16 : width + 32, :] = place_rows((16, cols), {0: lh, 1: lm, 2: ll}).astype(BF16)

        def l2_in(o):
            zp, dev = z_dev(o)
            remote(l2.at[k, zp], l2.at[k, zp], l2_send.at[k, zp], l2_recv.at[k, zp], dev).wait_recv()

        loop(nz, l2_in, 1)
        whole = l2[k, 0]
        for zp in range(1, nz):
            whole = whole + l2[k, zp]
        load = whole[: hrows * nz]
        tt_all = whole[hrows * nz :]
        cap = cap_s[...]
        mu_s[...] = jnp.maximum(0.0, mu_s[...] + size * (load - cap) / (load + cap))
        loop(nz, build_extra)
        tf[g] = tt_all

        loop(nx, lambda o: l1_copy(o).wait_send(), 1)
        loop(ng, lambda o: c_copy(o).wait_send(), 1)
        loop(nz, lambda o: l2_copy(o).wait_send(), 1)

    tt[...] = jnp.zeros((8, 128), F32)
    loop(ITERS, step)

    for yp in range(ny):
        row = lam_s[pl.ds(yp * CORES + core, 1), :]
        for j in range(crows):
            fin[z, yp * crows + j : yp * crows + j + 1, :] = row[:, 128 * j : 128 * (j + 1)]

    def fin_copy(o):
        zp, dev = z_dev(near(o, nz))
        return remote(fin.at[z], fin.at[z], fin_send.at[zp], fin_recv.at[z], dev)

    loop(nz, lambda o: fin_copy(o).start(), 1)
    own_mu = mu_s[pl.ds(z * hrows, hrows), :]
    tf[g, ITERS : ITERS + hrows, :] = own_mu

    def tf_copy(o):
        gp, dev = g_dev(o)
        return remote(tf.at[g], tf.at[g], tf_send.at[gp], tf_recv.at[g], dev)

    loop(ng, lambda o: tf_copy(o).start(), 1)

    def tf_in(o):
        gp, dev = g_dev(o)
        remote(tf.at[gp], tf.at[gp], tf_send.at[gp], tf_recv.at[gp], dev).wait_recv()

    loop(ng, tf_in, 1)
    total = tf[0]
    for gp in range(1, ng):
        total = total + tf[gp]
    sums = jnp.sum(total, axis=1, keepdims=True) * (1.0 / total_cust)
    bound_out[...] = jnp.broadcast_to(sums, (8, 128))
    for h in range(CORES):
        mu_out[h * hrows : (h + 1) * hrows, :] = tf[y * CORES + h, ITERS : ITERS + hrows, :]

    def fin_in(o):
        zp, dev = z_dev(o)
        remote(fin.at[zp], fin.at[zp], fin_send.at[zp], fin_recv.at[zp], dev).wait_recv()

    loop(nz, fin_in, 1)
    for yp in range(ny):
        for zp in range(nz):
            first = (yp * nz + zp) * crows
            lam_out[first : first + crows, :] = fin[zp, yp * crows : (yp + 1) * crows, :]

    loop(nz, lambda o: fin_copy(o).wait_send(), 1)
    loop(ng, lambda o: tf_copy(o).wait_send(), 1)


def local(dims, fac_coords, cust_coords, open_flags, demand, fixed_cost, capacity, cap_mult, cover_mult):
    ny, nz, nx = dims
    ng = ny * CORES
    fac_n, width = fac_coords.shape
    half = fac_n // CORES
    cols = cust_coords.shape[0]
    hrows = half // 128
    crows = cols // 128
    lrows = hrows * nz + 8
    assert hrows * 4 <= 8 and ITERS + hrows <= 8 and lrows % 8 == 0
    view = lambda a: a.reshape(-1, 128)
    vmem = pl.BlockSpec(memory_space=pltpu.VMEM)
    dma = pltpu.SemaphoreType.DMA
    lam, mu, bounds = pl.pallas_call(
        functools.partial(kernel, ny, nz, nx),
        out_shape=(
            jax.ShapeDtypeStruct((demand.shape[0] // 128, 128), F32),
            jax.ShapeDtypeStruct((fac_n // 128, 128), F32),
            jax.ShapeDtypeStruct((8, 128), F32),
        ),
        in_specs=[vmem] * 8,
        out_specs=(vmem,) * 3,
        scratch_shapes=[
            pltpu.VMEM((nz, half, width), BF16),
            pltpu.VMEM((nz, half, 128), BF16),
            pltpu.VMEM((ng, width + 128, cols), BF16),
            pltpu.VMEM((nz, 8, 128), F32),
            pltpu.VMEM((ng, 8, cols), F32),
            pltpu.VMEM((half, cols), F32),
            pltpu.VMEM((half, cols), F32),
            pltpu.VMEM((nz, half, 128), F32),
            pltpu.VMEM((ng, 8, cols), F32),
            pltpu.VMEM((ng, 8, cols), F32),
            pltpu.VMEM((ng, cols), F32),
            pltpu.VMEM((hrows * nz, 128), F32),
            pltpu.VMEM((hrows * nz, 128), F32),
            pltpu.VMEM((hrows * nz, 128), F32),
            pltpu.VMEM((8, 128), F32),
            pltpu.VMEM((ITERS, ng, ng, cols), F32),
            pltpu.VMEM((ITERS, nx, lrows, 128), F32),
            pltpu.VMEM((ITERS, nz, lrows, 128), F32),
            pltpu.VMEM((nz, ny * crows, 128), F32),
            pltpu.VMEM((ng, 8, 128), F32),
            dma((nz,)), dma((nz,)), dma((nz,)), dma((nz,)), dma((ng,)), dma((ng,)), dma((ny,)),
            dma((ITERS, ng)), dma((ITERS, ng)), dma((ITERS, nx)), dma((ITERS, nx)),
            dma((ITERS, nz)), dma((ITERS, nz)), dma((nz,)), dma((nz,)), dma((ng,)), dma((ng,)),
        ],
        compiler_params=pltpu.CompilerParams(
            collective_id=0, has_side_effects=True, vmem_limit_bytes=48 * 1024 * 1024
        ),
        name="dual",
    )(
        fac_coords, cust_coords, view(open_flags), view(demand), view(fixed_cost), view(capacity),
        view(cap_mult), view(cover_mult),
    )
    return lam.reshape(-1), mu.reshape(-1), bounds[:ITERS, 0]


def solution(mesh, dims=(4, 8, 4)):
    return jax.shard_map(
        functools.partial(local, dims),
        mesh=mesh,
        in_specs=(
            P("fac", None),
            P(("cust", "fac"), None),
            P("fac"),
            P("cust"),
            P("fac"),
            P("fac"),
            P("fac"),
            P("cust"),
        ),
        out_specs=(P("cust"), P("fac"), P()),
        check_vma=False,
    )
```

time: 479 us -> 129 us (0.27)
  waiting for transfers between devices: 210 us -> 0 us
  matrix products: 157 us -> 0 us
  Pallas kernels: 0 us -> 122 us
  starting transfers between devices: 34.8 us -> 0 us
  other arithmetic: 19.2 us -> 0 us
  local copies, waits for them, and re-layouts: 23.9 us -> 6.02 us
  between operations: 18.2 us -> 0.68 us
  blocking collectives: 13.3 us -> 0 us
    dot_general x24 -> x0, matrix products: 157 us -> none  [one_block(): lax.dot_general(fac_coords, cols, (((1,), (1,)), ((), ())), preferred_ele...]
    all_to_all x6 -> x0, waiting for transfers between devices: 156 us -> none  [copy_for_each(): lax.all_to_all(jnp.broadcast_to(x[None], (size, *x.shape)), axis, 0, 0, t...]
    pallas_call x0 -> x1, Pallas kernels: none -> 122 us  [local(): pl.pallas_call(functools.partial(kernel, ny, nz, nx), out_shape=(jax.Shap...]
    all_gather x1 -> x0, waiting for transfers between devices: 53.8 us -> none  [stacked_from(): blocks = lax.all_gather(blocks, axes[k])]
    all_to_all x6 -> x0, starting transfers between devices: 34.7 us -> none  [copy_for_each(): lax.all_to_all(jnp.broadcast_to(x[None], (size, *x.shape)), axis, 0, 0, t...]
    all_gather x1 -> x0, blocking collectives: 13.3 us -> none  [stacked_from(): blocks = lax.all_gather(blocks, axes[k])]
    reduce_sum x11 -> x0, other arithmetic: 9.79 us -> none  [the longest x6 3.73 us: of_everyone(): return jnp.sum(everything, axis=0)]
    broadcast_in_dim x6 -> x0, local copies, waits for them, and re-layouts: 9.18 us -> none  [copy_for_each(): jnp.broadcast_to(x[None], (size, *x.shape))]
  transfers between devices with their start and end apart: 7 -> 0, of which waited for: 7 -> 0; matrix products, arithmetic and copies ran while one was open for 2% -> 0% of each run, Pallas kernels for 0% -> 0%
where the time goes in v1:
time: 129 us; the launch traced here: 128 us
  Pallas kernels  122 us (95%)
  local copies, waits for them, and re-layouts  6.02 us (5%)
    pallas_call x1, Pallas kernels, local(): pl.pallas_call(functools.partial(kernel, ny, nz, nx), out_shape=(jax.Shap...  122 us
    unnamed x18, local copies, waits for them, and re-layouts  5.39 us

profile of v1, /device:TPU:1, one launch (start us, length us, event | category | flops | bytes accessed | tf_op | source)
XLA Modules:
  0.0 128.3 jit_solution(5380366244633396348)
XLA Ops:
  0.6 0.0 copy-start.7
  0.6 0.0 copy-start.6
  0.7 0.0 copy-start.5
  0.7 0.0 copy-start.4
  0.7 0.6 copy-done.7
  1.3 0.0 copy-done.6
  1.3 0.0 copy-done.5
  1.3 0.0 copy-done.4
  1.4 0.0 copy-start
  1.4 0.9 copy-done
  2.3 0.0 copy-start.1
  2.3 0.9 copy-done.1
  3.2 0.0 copy-start.2
  3.2 0.8 copy-done.2
  4.0 0.0 copy-start.3
  4.0 0.8 copy-done.3
  4.9 121.6 %dual.1 = (f32[128,128]{1,0:T(8,128)S(1)}, f32[4,128]{1,0:T(4,128)S(1)}, f32[8,128]{1,0:T(8,128)S(1)}) custom-call(bf16[512,128]{1,0:T(8,128)(2,1)S(1)} %copy-done, bf16[512,128]{1,0:T(8,128)(2,1)S(1)} %copy-done.1, s32[4,128]{1,0:T(4,128)S(1)} %bitcast.11, s32[128,128]{1,0:T(8,128)S(1)} %bitcast.8, f32[4,128]{1,0:T(4,128)S(1)} %bitcast.12, ...), custom_call_target="tpu_custom_call" | custom-call | tf_op jit(solution)/shard_map/dual/pallas_call | solution.py:410
  126.5 0.6 slice_reduce_fusion
  127.1 0.6 copy.13
  127.7 0.6 copy.14
Async XLA Ops:
  0.6 0.7 copy-start.7
  0.6 0.7 copy-start.6
  0.7 0.7 copy-start.5
  0.7 0.7 copy-start.4
  1.4 0.9 copy-start
  2.3 0.9 copy-start.1
  3.2 0.8 copy-start.2
  4.0 0.8 copy-start.3
